TPU v7x, 256 devices: a whole 4x4x8 slice. The times are simulated.
256 devices in a mesh: dp: 2 (over core), expert: 128 (over z, x, y).
Axes of the slice: x: 4, y: 4, z: 8, core: 2. Of those that a mesh axis runs over, the one named last changes fastest.
Arguments:
- tokens: bfloat16 [65536, 1024], P(('dp', 'expert')), may hold values from -6 to 6
- ln_gain: float32 [1024], replicated, may hold values from 0.5 to 1.5
- router_weight: bfloat16 [1024, 128], replicated
- routes_expert: int32 [65536], P(('dp', 'expert')), may hold values from 0 to 127, as said below
- route_slot: int32 [65536], P(('dp', 'expert')), may hold values from -1 to 3, as said below
- w_in: bfloat16 [128, 1024, 4096], P('expert', None, 'dp'), may hold values from -0.1875 to 0.1875
- w_out: bfloat16 [128, 4096, 1024], P('expert', 'dp'), may hold values from -0.09375 to 0.09375
Outputs:
- mixed: bfloat16 [65536, 1024], P(('dp', 'expert'))
- expert_update: bfloat16 [65536, 1024], P(('dp', 'expert'))
Inputs may be any that keep to these rules, and one draw needn't show every extreme that they name: `routes_expert`: every expert is chosen by some token. route_slot[t] is the number of earlier tokens of the same device (the same aligned block of 256 tokens) routed to the same expert, or -1 where that number is 4 or more; the value 4 - 1 occurs in every draw.
All inputs are finite; a program needn't handle non-finite values.
Results may differ from a plain program's by a relative error of at most 0.0058.
Values may be sent and summed in bfloat16 or wider, within the bound.
A program may use at most 64 MiB of HBM per device.

v0:
```python
import jax
import jax.numpy as jnp
from jax import lax
from jax.sharding import PartitionSpec as P

CAP = 4


def from_everyone(x, axis):
    count = lax.axis_size(axis)
    return lax.all_to_all(jnp.broadcast_to(x[None], (count, *x.shape)), axis, 0, 0, tiled=True)


def in_order(tiles, dim):
    dims = list(tiles.shape[1:])
    dims[dim] *= tiles.shape[0]
    return jnp.moveaxis(tiles, 0, dim).reshape(dims)


def collect(x, axis, dim):
    tiles = from_everyone(x, axis)
    return in_order(tiles, dim)


def cut_along(x, dim, count):
    dims = x.shape
    tiles = x.reshape(*dims[:dim], count, dims[dim] // count, *dims[dim + 1 :])
    return jnp.moveaxis(tiles, dim, 0)


def sent_and_summed(x, axis, dim):
    tiles = cut_along(x, dim, lax.axis_size(axis))
    arrived = lax.all_to_all(tiles, axis, split_axis=0, concat_axis=0, tiled=True)
    return arrived.sum(axis=0)


def expert_rows(rows, weight_in, weight_out):
    hidden = jax.nn.gelu(
        jnp.einsum("sxcd,xdh->sxch", rows, weight_in, preferred_element_type=jnp.float32),
        approximate=True,
    ).astype(jnp.bfloat16)
    return jnp.einsum("sxch,xhd->sxcd", hidden, weight_out, preferred_element_type=jnp.float32)


def per_device(tokens, ln_gain, router_weight, routes_expert, route_slot, w_in, w_out):
    width = tokens.shape[1]
    values = tokens.astype(jnp.float32)
    mean = jnp.mean(values, axis=1, keepdims=True)
    var = jnp.mean((values - mean) ** 2, axis=1, keepdims=True)
    normed = ((values - mean) * lax.rsqrt(var + 1e-06) * ln_gain[None, :]).astype(jnp.bfloat16)
    logits = jnp.dot(normed, router_weight, preferred_element_type=jnp.float32)
    probs = jax.nn.softmax(logits, axis=1)
    expert_count = router_weight.shape[1]
    columns = jnp.arange(expert_count, dtype=jnp.int32)
    gate = jnp.sum(jnp.where(routes_expert[:, None] == columns[None, :], probs, 0.0), axis=1)
    kept = route_slot >= 0
    slot_rows = expert_count * CAP
    flat = jnp.where(kept, routes_expert * CAP + route_slot, slot_rows)
    outgoing = jnp.zeros((slot_rows, width), jnp.bfloat16).at[flat].set(normed, mode="drop")
    outgoing = outgoing.reshape(expert_count, CAP, width)
    local_experts = w_in.shape[0]
    block = lax.all_to_all(outgoing, "expert", split_axis=0, concat_axis=0, tiled=True)
    slots_here = block.shape[1]
    both_groups = collect(block, "dp", 0)
    rows = both_groups.reshape(-1, local_experts, slots_here, width)
    partial_value = expert_rows(rows, w_in, w_out).reshape(-1, slots_here, width)
    summed = sent_and_summed(partial_value, "dp", 0).astype(jnp.bfloat16)
    returned = lax.all_to_all(summed, "expert", split_axis=0, concat_axis=0, tiled=True)
    back = returned.reshape(slot_rows, width)[jnp.minimum(flat, slot_rows - 1)]
    update = jnp.where(kept[:, None], back, jnp.zeros_like(back))
    mixed = (values + gate[:, None] * update.astype(jnp.float32)).astype(jnp.bfloat16)
    return (mixed, update)


def solution(mesh):
    in_specs = (
        P(("dp", "expert"), None),
        P(),
        P(),
        P(("dp", "expert")),
        P(("dp", "expert")),
        P("expert", None, "dp"),
        P("expert", "dp", None),
    )
    out_specs = (P(("dp", "expert"), None), P(("dp", "expert"), None))
    return jax.shard_map(
        per_device, mesh=mesh, in_specs=in_specs, out_specs=out_specs, check_vma=False
    )
```

profile of v0, /device:TPU:1, one launch (start us, length us, event | category | flops | bytes accessed | tf_op | source)
XLA Modules:
  0.0 129.2 jit_solution(6435346491169810587)
XLA Ops:
  0.6 0.0 copy-start
  0.6 1.2 convert_reduce_fusion
  1.9 1.3 %fusion.22 = f32[256]{0:T(256)S(1)} fusion(bf16[256,1024]{1,0:T(8,128)(2,1)} %param.7, f32[256]{0:T(256)S(1)} %broadcast_multiply_fusion), kind=kLoop, calls=%fused_computation.24 | loop fusion | flops 1048320 | bytes 526336 | tf_op jit(solution)/shard_map/reduce_sum | solution.py:49
  3.2 0.7 compare_select_fusion
  3.9 2.6 %scatter_custom_fusion = bf16[512,1024]{1,0:T(8,128)(2,1)S(1)} fusion(s32[256]{0:T(256)S(1)} %get-tuple-element.5, bf16[]{:T(256)} %constant.4.clone.1, bf16[256,1024]{1,0:T(8,128)(2,1)} %param.7, f32[1024]{0:T(1024)} %param.8, f32[256]{0:T(256)S(1)} %add_rsqrt_fusion, f32[256]{0:T(256)S(1)} %broadcast_multiply_fusion), kind=kCustom, calls=%fused_computation.28 | custom fusion | flops 1310720 | bytes 1579010 | tf_op jit(solution)/shard_map/scatter | solution.py:59
  6.6 0.4 reshape.44
  7.0 44.9 %all_to_all.20 = bf16[128,4,1024]{2,1,0:T(4,128)(2,1)S(1)} all-to-all(bf16[128,4,1024]{2,1,0:T(4,128)(2,1)S(1)} %reshape.44), channel_id=1, replica_groups=mesh['dp'=2,'expert'=128] {'expert'}, dimensions={0} | all-to-all | bytes 2097152 | tf_op jit(solution)/shard_map/all_to_all | solution.py:62
  51.9 0.3 copy.15
  52.2 0.3 broadcast_in_dim.48
  52.4 8.5 %all_to_all.21 = bf16[2,128,4,1024]{3,1,2,0:T(8,128)(2,1)S(1)} all-to-all(bf16[2,128,4,1024]{3,1,2,0:T(8,128)(2,1)S(1)} %broadcast_in_dim.48), channel_id=1, replica_groups=mesh['dp'=2,'expert'=128] {'dp'}, dimensions={0} | all-to-all | bytes 4194304 | tf_op jit(solution)/shard_map/all_to_all | solution.py:11
  61.0 0.2 copy.16
  61.2 14.4 %fusion.8 = f32[256,4,1024]{2,0,1:T(8,128)} fusion(bf16[1,2048,1024]{2,1,0:T(8,128)(2,1)} %param.13, bf16[256,4,1024]{2,0,1:T(8,128)(2,1)S(1)} %bitcast.36, bf16[1,1024,2048]{2,1,0:T(8,128)(2,1)} %param.12), kind=kOutput, calls=%fused_computation.11 | convolution fusion | flops 8608808960 | bytes 14680064 | tf_op jit(solution)/shard_map/sxch,xhd->sxcd/dot_general | solution.py:42
  75.6 2.5 %copy.17 = f32[2,128,4,1024]{3,1,2,0:T(8,128)S(1)} copy(f32[2,128,4,1024]{3,1,0,2:T(8,128)} %bitcast.35) | data formatting | bytes 8388608 | tf_op jit(solution)/shard_map/reshape;reshape | solution.py:27
  78.1 8.1 %all_to_all.22 = f32[2,128,4,1024]{3,1,2,0:T(8,128)} all-to-all(f32[2,128,4,1024]{3,1,2,0:T(8,128)S(1)} %copy.17), channel_id=1, replica_groups=mesh['dp'=2,'expert'=128] {'dp'}, dimensions={0} | all-to-all | bytes 8388608 | tf_op jit(solution)/shard_map/all_to_all | solution.py:33
  86.2 0.0 copy-start.1
  86.2 0.0 copy-start.2
  86.2 0.0 copy-start.3
  86.2 2.8 %reduce_sum.49 = bf16[128,4,1024]{2,0,1:T(8,128)(2,1)S(1)} reduce(f32[2,128,4,1024]{3,1,2,0:T(8,128)} %all_to_all.22, f32[]{:T(128)} %constant.13.clone.1), dimensions={0}, to_apply=%region_6.7 | reduce | flops 524288 | bytes 5242884 | tf_op jit(solution)/shard_map/reduce_sum | solution.py:34
  89.0 0.0 copy-start.4
  89.0 1.8 %copy.19 = bf16[128,4,1024]{2,1,0:T(4,128)(2,1)} copy(bf16[128,4,1024]{2,0,1:T(8,128)(2,1)S(1)} %reduce_sum.49) | data formatting | bytes 2097152 | tf_op jit(solution)/shard_map/convert_element_type | solution.py:67
  90.8 6.2 %all-to-all-start.3 = ((bf16[128,4,1024]{2,1,0:T(4,128)(2,1)}), bf16[128,4,1024]{2,1,0:T(4,128)(2,1)S(1)}, u32[]{:S(2)}, u32[]{:S(2)}) async-start(bf16[128,4,1024]{2,1,0:T(4,128)(2,1)} %copy.19), calls=%async_computation.3 | async-start | bytes 2097152 | tf_op jit(solution)/shard_map/all_to_all | solution.py:68
  97.0 0.0 copy-done
  97.0 0.0 copy-done.1
  97.0 0.0 copy-done.2
  97.1 0.4 fusion.36
  97.5 0.0 copy-done.3
  97.5 0.1 select_reduce_fusion
  97.6 0.0 copy-done.4
  97.6 28.9 %all-to-all-done.3 = bf16[128,4,1024]{2,1,0:T(4,128)(2,1)S(1)} async-done(((bf16[128,4,1024]{2,1,0:T(4,128)(2,1)}), bf16[128,4,1024]{2,1,0:T(4,128)(2,1)S(1)}, u32[]{:S(2)}, u32[]{:S(2)}) %all-to-all-start.3) | async-done | bytes 1048608 | tf_op jit(solution)/shard_map/all_to_all | solution.py:68
  126.5 0.3 reshape.49
  126.8 1.2 gather_fusion
  128.0 1.2 fusion.25
  (5 shorter events, 0.1 us)
Async XLA Ops:
  0.6 96.4 %copy-start = (bf16[1024,128]{1,0:T(8,128)(2,1)S(1)}, bf16[1024,128]{1,0:T(8,128)(2,1)}, u32[]{:S(2)}) copy-start(bf16[1024,128]{1,0:T(8,128)(2,1)} %param.9) | copy-start | bytes 786436
  86.2 10.9 %copy-start.1 = (bf16[256,1024]{1,0:T(8,128)(2,1)S(1)}, bf16[256,1024]{1,0:T(8,128)(2,1)}, u32[]{:S(2)}) copy-start(bf16[256,1024]{1,0:T(8,128)(2,1)} %param.7) | copy-start | bytes 1572868
  86.2 10.9 %copy-start.2 = (f32[1024]{0:T(1024)S(1)}, f32[1024]{0:T(1024)}, u32[]{:S(2)}) copy-start(f32[1024]{0:T(1024)} %param.8) | copy-start | bytes 12292
  86.2 11.4 %copy-start.3 = (s32[256]{0:T(256)S(1)}, s32[256]{0:T(256)}, u32[]{:S(2)}) copy-start(s32[256]{0:T(256)} %param.10) | copy-start | bytes 3076
  89.0 8.6 %copy-start.4 = (s32[256]{0:T(256)S(1)}, s32[256]{0:T(256)}, u32[]{:S(2)}) copy-start(s32[256]{0:T(256)} %param.11) | copy-start | bytes 3076
  90.8 35.7 %all-to-all-start.3 = ((bf16[128,4,1024]{2,1,0:T(4,128)(2,1)}), bf16[128,4,1024]{2,1,0:T(4,128)(2,1)S(1)}, u32[]{:S(2)}, u32[]{:S(2)}) async-start(bf16[128,4,1024]{2,1,0:T(4,128)(2,1)} %copy.19), calls=%async_computation.3 | async-start | bytes 2097152 | tf_op jit(solution)/shard_map/all_to_all | solution.py:68
where the time goes:
time: 130 us; the launch traced here: 129 us
  blocking collectives  61.5 us (47%)
  waiting for transfers between devices  28.9 us (22%)
  matrix products  14.8 us (11%)
  other arithmetic  10 us (8%)
  local copies, waits for them, and re-layouts  7 us (5%)
  starting transfers between devices  6.19 us (5%)
    all_to_all x1, blocking collectives, per_device(): lax.all_to_all(outgoing, 'expert', split_axis=0, concat_axis=0, tiled=True)  44.9 us
    all_to_all x1, waiting for transfers between devices, per_device(): lax.all_to_all(summed, 'expert', split_axis=0, concat_axis=0, tiled=True)  28.9 us
    dot_general x1, matrix products, expert_rows(): jnp.einsum('sxch,xhd->sxcd', hidden, weight_out, preferred_element_type=j...  14.4 us
    all_to_all x1, blocking collectives, from_everyone(): lax.all_to_all(jnp.broadcast_to(x[None], (count, *x.shape)), axis, 0, 0,...  8.51 us
    all_to_all x1, blocking collectives, sent_and_summed(): lax.all_to_all(tiles, axis, split_axis=0, concat_axis=0, tiled=True)  8.11 us
    all_to_all x1, starting transfers between devices, per_device(): lax.all_to_all(summed, 'expert', split_axis=0, concat_axis=0, tiled=True)  6.19 us
    reduce_sum x1, other arithmetic, sent_and_summed(): return arrived.sum(axis=0)  2.82 us
    scatter x1, other arithmetic, per_device(): jnp.zeros((slot_rows, width), jnp.bfloat16).at[flat]  2.62 us
  transfers between devices with their start and end apart: 1, of which 1 were waited for; matrix products, arithmetic and copies ran while one was open for 0% of the time, Pallas kernels for 0%

commit v1 on v0

v1 whole, which is shorter than its diff:
```python
import functools

import jax
import jax.numpy as jnp
from jax import lax
from jax.experimental import pallas as pl
from jax.experimental.pallas import tpu as pltpu
from jax.sharding import PartitionSpec as P

CAP = 4
ZS, XS, YS = 8, 4, 4
PLANE = XS * YS
EXPERTS = ZS * PLANE
SLOTS = EXPERTS * CAP
CHUNKS = ((3, 5), (2, 6), (4, 0), (1, 7))
ORDER = tuple(dz for pair in CHUNKS for dz in pair)
SELF = ORDER.index(0) * PLANE
CHUNK_BLOCKS = 2 * PLANE
CHUNK_ROWS = CHUNK_BLOCKS * CAP
TILE = 512
MESH = pl.DeviceIdType.MESH


def kernel(
    tokens, gain, router, experts, slots, w_in, w_out,
    mixed, update,
    send, recv, resp, back, win, wout, normed, acc, gate, onehot,
    load_sem, pair_send, pair_recv, out_send, out_recv, back_send, back_recv,
):
    core = lax.axis_index("dp")
    me = lax.axis_index("expert")
    z, x, y = me // PLANE, lax.rem(me // YS, XS), lax.rem(me, YS)
    half = w_in.shape[2] // TILE

    def at(expert):
        return {"dp": core, "expert": expert}

    def away(dz, j, sign):
        dx, dy = j // YS, lax.rem(j, YS)
        return (
            lax.rem(z + sign * dz + ZS, ZS) * PLANE
            + lax.rem(x + sign * dx + XS, XS) * YS
            + lax.rem(y + sign * dy + YS, YS)
        )

    def blocks(chunk, act):
        for i, dz in enumerate(CHUNKS[chunk]):
            base = (2 * chunk + i) * PLANE

            def step(j, carry):
                act(base + j, dz, j)
                return carry

            lax.fori_loop(1 if dz == 0 else 0, PLANE, step, 0)

    def greet(k, dz, j):
        pl.semaphore_signal(barrier, inc=1, device_id=at(away(dz, j, 1)), device_id_type=MESH)

    loads = []
    for t in range(half):
        cols = pl.ds(t * TILE, TILE)
        loads.append(pltpu.make_async_copy(w_in.at[0, :, cols], win.at[t], load_sem.at[0, t]))
        loads.append(pltpu.make_async_copy(w_out.at[0, cols, :], wout.at[t], load_sem.at[1, t]))
    for copy in loads:
        copy.start()

    barrier = pltpu.get_barrier_semaphore()
    partner = {"dp": 1 - core, "expert": me}
    pl.semaphore_signal(barrier, inc=1, device_id=partner, device_id_type=MESH)
    for chunk in range(len(CHUNKS)):
        blocks(chunk, greet)

    values = tokens[...].astype(jnp.float32)
    mean = jnp.mean(values, axis=1, keepdims=True)
    centred = values - mean
    var = jnp.mean(centred * centred, axis=1, keepdims=True)
    normed[...] = (centred * lax.rsqrt(var + 1e-06) * gain[...]).astype(jnp.bfloat16)

    expert = experts[...]
    slot = slots[...]
    dz = (expert // PLANE - z) & (ZS - 1)
    dx = ((expert // YS) % XS - x) & (XS - 1)
    dy = (expert % YS - y) & (YS - 1)
    place = jnp.zeros_like(dz)
    for i, d in enumerate(ORDER):
        place = jnp.where(dz == d, i, place)
    rel = ((place * PLANE) + dx * YS + dy) * CAP + slot
    rel = jnp.where(slot >= 0, rel, -1)
    count = rel.shape[1]
    for chunk in range(len(CHUNKS)):
        rows = lax.broadcasted_iota(jnp.int32, (CHUNK_ROWS, count), 0) + chunk * CHUNK_ROWS
        pick = jnp.where(rows == rel, 1.0, 0.0).astype(jnp.bfloat16)
        picked = jnp.dot(pick, normed[...], preferred_element_type=jnp.float32)
        first = chunk * CHUNK_BLOCKS
        send[first : first + CHUNK_BLOCKS] = picked.reshape(CHUNK_BLOCKS, CAP, -1).astype(jnp.bfloat16)

    pl.semaphore_wait(barrier, EXPERTS)

    def pair_copy(w, t, which):
        dst = (win, wout)[which].at[half + t]
        src = w.at[0, :, pl.ds(t * TILE, TILE)] if which == 0 else w.at[0, pl.ds(t * TILE, TILE), :]
        return pltpu.make_async_remote_copy(
            src_ref=src, dst_ref=dst, send_sem=pair_send.at[which, t], recv_sem=pair_recv.at[which, t],
            device_id=partner, device_id_type=MESH,
        )

    def dispatch(chunk):
        def act(k, dz, j):
            pltpu.make_async_remote_copy(
                src_ref=send.at[k], dst_ref=recv.at[k], send_sem=out_send, recv_sem=out_recv.at[chunk],
                device_id=at(away(dz, j, 1)), device_id_type=MESH,
            ).start()

        blocks(chunk, act)

    pairs = []
    for chunk in range(len(CHUNKS)):
        dispatch(chunk)
        if chunk == 0:
            pairs = [pair_copy((w_in, w_out)[s], t, s) for t in range(half) for s in (0, 1)]
            for copy in pairs:
                copy.start()
    recv[SELF] = send[SELF]

    eye = lax.broadcasted_iota(jnp.int32, (count, count), 0) == lax.broadcasted_iota(jnp.int32, (count, count), 1)

    def column(row):
        return jnp.sum(jnp.where(eye, row.astype(jnp.float32), 0.0), axis=1, keepdims=True).astype(jnp.int32)

    expert_col, rel_col = column(expert), column(rel)
    logits = jnp.dot(normed[...], router[...], preferred_element_type=jnp.float32)
    powers = jnp.exp(logits - jnp.max(logits, axis=1, keepdims=True))
    lanes = lax.broadcasted_iota(jnp.int32, powers.shape, 1)
    chosen = jnp.sum(jnp.where(lanes == expert_col, powers, 0.0), axis=1, keepdims=True)
    gate[...] = jnp.broadcast_to(chosen / jnp.sum(powers, axis=1, keepdims=True), gate.shape)
    for chunk in range(len(CHUNKS)):
        cols = lax.broadcasted_iota(jnp.int32, (count, CHUNK_ROWS), 1) + chunk * CHUNK_ROWS
        onehot[chunk] = jnp.where(cols == rel_col, 1.0, 0.0).astype(jnp.bfloat16)

    for copy in loads:
        copy.wait()

    def whole(src, dst, chunk, send_sem, recv_sem):
        first = chunk * CHUNK_BLOCKS
        many = CHUNK_BLOCKS - (1 if 0 in CHUNKS[chunk] else 0)
        return pltpu.make_async_remote_copy(
            src_ref=src.at[pl.ds(first, many)], dst_ref=dst.at[pl.ds(first, many)],
            send_sem=send_sem, recv_sem=recv_sem, device_id=partner, device_id_type=MESH,
        )

    for chunk in range(len(CHUNKS)):
        whole(send, recv, chunk, out_send, out_recv.at[chunk]).wait_recv()
        if chunk == 0:
            for copy in pairs:
                copy.wait_recv()
        first = chunk * CHUNK_BLOCKS
        here = recv[first : first + CHUNK_BLOCKS].reshape(CHUNK_ROWS, -1)
        acc[...] = jnp.zeros_like(acc)

        def tile(t, carry):
            hidden = jnp.dot(here, win[t], preferred_element_type=jnp.float32)
            inner = 0.7978845608028654 * (hidden + 0.044715 * (hidden * hidden * hidden))
            hidden = (hidden * (0.5 * (1.0 + jnp.tanh(inner)))).astype(jnp.bfloat16)
            acc[...] += jnp.dot(hidden, wout[t], preferred_element_type=jnp.float32)
            return carry

        lax.fori_loop(0, 2 * half, tile, 0)
        resp[first : first + CHUNK_BLOCKS] = acc[...].reshape(CHUNK_BLOCKS, CAP, -1).astype(jnp.bfloat16)

        def answer(k, dz, j):
            pltpu.make_async_remote_copy(
                src_ref=resp.at[k], dst_ref=back.at[k], send_sem=back_send, recv_sem=back_recv.at[chunk],
                device_id=at(away(dz, j, -1)), device_id_type=MESH,
            ).start()

        blocks(chunk, answer)
    back[SELF] = resp[SELF]

    total = jnp.zeros(values.shape, jnp.float32)
    for chunk in range(len(CHUNKS)):
        whole(resp, back, chunk, back_send, back_recv.at[chunk]).wait_recv()
        first = chunk * CHUNK_BLOCKS
        rows = back[first : first + CHUNK_BLOCKS].reshape(CHUNK_ROWS, -1)
        total = total + jnp.dot(onehot[chunk], rows, preferred_element_type=jnp.float32)
    update[...] = total.astype(jnp.bfloat16)
    mixed[...] = (tokens[...].astype(jnp.float32) + gate[:, :1] * total).astype(jnp.bfloat16)

    for copy in pairs:
        copy.wait_send()
    for chunk in range(len(CHUNKS)):
        whole(send, recv, chunk, out_send, out_recv.at[chunk]).wait_send()
        whole(resp, back, chunk, back_send, back_recv.at[chunk]).wait_send()


def per_device(tokens, ln_gain, router_weight, routes_expert, route_slot, w_in, w_out):
    count, width = tokens.shape
    half = w_in.shape[2] // TILE
    vmem = pl.BlockSpec(memory_space=pltpu.VMEM)
    hbm = pl.BlockSpec(memory_space=pl.ANY)
    blocks = (EXPERTS, CAP, width)
    dma = pltpu.SemaphoreType.DMA
    return pl.pallas_call(
        kernel,
        out_shape=(jax.ShapeDtypeStruct(tokens.shape, jnp.bfloat16),) * 2,
        in_specs=[vmem] * 5 + [hbm] * 2,
        out_specs=(vmem, vmem),
        scratch_shapes=[
            pltpu.VMEM(blocks, jnp.bfloat16),
            pltpu.VMEM(blocks, jnp.bfloat16),
            pltpu.VMEM(blocks, jnp.bfloat16),
            pltpu.VMEM(blocks, jnp.bfloat16),
            pltpu.VMEM((2 * half, width, TILE), jnp.bfloat16),
            pltpu.VMEM((2 * half, TILE, width), jnp.bfloat16),
            pltpu.VMEM((count, width), jnp.bfloat16),
            pltpu.VMEM((CHUNK_ROWS, width), jnp.float32),
            pltpu.VMEM((count, 128), jnp.float32),
            pltpu.VMEM((len(CHUNKS), count, CHUNK_ROWS), jnp.bfloat16),
            dma((2, half)), dma((2, half)), dma((2, half)),
            dma, dma((len(CHUNKS),)), dma, dma((len(CHUNKS),)),
        ],
        compiler_params=pltpu.CompilerParams(
            collective_id=0, has_side_effects=True, vmem_limit_bytes=56 * 1024 * 1024
        ),
    )(
        tokens, ln_gain.reshape(1, -1), router_weight,
        routes_expert.reshape(1, -1), route_slot.reshape(1, -1), w_in, w_out,
    )


def solution(mesh):
    in_specs = (
        P(("dp", "expert"), None),
        P(),
        P(),
        P(("dp", "expert")),
        P(("dp", "expert")),
        P("expert", None, "dp"),
        P("expert", "dp", None),
    )
    out_specs = (P(("dp", "expert"), None), P(("dp", "expert"), None))
    return jax.shard_map(
        per_device, mesh=mesh, in_specs=in_specs, out_specs=out_specs, check_vma=False
    )
```

time: 130 us -> 69.7 us (0.54)
  Pallas kernels: 0 us -> 65.1 us
  blocking collectives: 61.5 us -> 0 us
  waiting for transfers between devices: 28.9 us -> 0 us
  matrix products: 14.8 us -> 0 us
  other arithmetic: 10 us -> 0 us
  starting transfers between devices: 6.19 us -> 0 us
  local copies, waits for them, and re-layouts: 7 us -> 3.74 us
    pallas_call x0 -> x1, Pallas kernels: none -> 65.1 us  [per_device(): pl.pallas_call(kernel, out_shape=(jax.ShapeDtypeStruct(tokens.shape, jnp....]
    all_to_all x3 -> x0, blocking collectives: 61.5 us -> none  [the longest x1 44.9 us: per_device(): lax.all_to_all(outgoing, 'expert', split_axis=0, concat_axis=0, tiled=True)]
    all_to_all x1 -> x0, waiting for transfers between devices: 28.9 us -> none  [per_device(): lax.all_to_all(summed, 'expert', split_axis=0, concat_axis=0, tiled=True)]
    dot_general x2 -> x0, matrix products: 14.8 us -> none  [the longest x1 14.4 us: expert_rows(): jnp.einsum('sxch,xhd->sxcd', hidden, weight_out, preferred_element_type=j...]
    all_to_all x1 -> x0, starting transfers between devices: 6.19 us -> none  [per_device(): lax.all_to_all(summed, 'expert', split_axis=0, concat_axis=0, tiled=True)]
    reduce_sum x5 -> x0, other arithmetic: 5.48 us -> none  [the longest x1 2.82 us: sent_and_summed(): return arrived.sum(axis=0)]
    unnamed x10 -> x2, local copies, waits for them, and re-layouts: 0.03 us -> 3.74 us
    scatter x1 -> x0, other arithmetic: 2.62 us -> none  [per_device(): jnp.zeros((slot_rows, width), jnp.bfloat16).at[flat]]
  transfers between devices with their start and end apart: 1 -> 0, of which waited for: 1 -> 0; matrix products, arithmetic and copies ran while one was open for 0% -> 0% of each run, Pallas kernels for 0% -> 0%
where the time goes in v1:
time: 69.7 us; the launch traced here: 69.5 us
  Pallas kernels  65.1 us (93%)
  local copies, waits for them, and re-layouts  3.74 us (5%)
    pallas_call x1, Pallas kernels, per_device(): pl.pallas_call(kernel, out_shape=(jax.ShapeDtypeStruct(tokens.shape, jnp....  65.1 us
    unnamed x2, local copies, waits for them, and re-layouts  3.74 us

profile of v1, /device:TPU:1, one launch (start us, length us, event | category | flops | bytes accessed | tf_op | source)
XLA Modules:
  0.0 69.5 jit_solution(6710790836982255219)
XLA Ops:
  0.6 65.1 %shard_map.86 = (bf16[256,1024]{1,0:T(8,128)(2,1)}, bf16[256,1024]{1,0:T(8,128)(2,1)}) custom-call(bf16[256,1024]{1,0:T(8,128)(2,1)} %tokens.1, f32[1,1024]{1,0:T(1,128)} %bitcast.3, bf16[1024,128]{1,0:T(8,128)(2,1)} %router.1, s32[1,256]{1,0:T(1,128)} %bitcast.4, s32[1,256]{1,0:T(1,128)} %bitcast.5, bf16[1,1024,2048]{2,1,0:T(8,128)(2,1)} %w_in.1, ...), custom_call_target="tpu_custom_call" | custom-call | tf_op jit(solution)/shard_map/pallas_call | solution.py:202
  65.8 1.9 %copy.11 = bf16[256,1024]{1,0:T(8,128)(2,1)} copy(bf16[256,1024]{1,0:T(8,128)(2,1)} %get-tuple-element.4) | data formatting | bytes 1048576
  67.6 1.9 %copy.12 = bf16[256,1024]{1,0:T(8,128)(2,1)} copy(bf16[256,1024]{1,0:T(8,128)(2,1)} %get-tuple-element.5) | data formatting | bytes 1048576

commit v2 on v1

--- a/solution.py
+++ b/solution.py
@@ -22,10 +22,11 @@
 
 
 def kernel(
-    tokens, gain, router, experts, slots, w_in, w_out,
-    mixed, update,
-    send, recv, resp, back, win, wout, normed, acc, gate, onehot,
-    load_sem, pair_send, pair_recv, out_send, out_recv, back_send, back_recv,
+    tokens_in, gain_in, router_in, experts_in, slots_in, w_in, w_out,
+    update, gate,
+    tokens, gain, router, experts, slots,
+    send, recv, resp, back, win, wout, normed, acc, onehot,
+    small_sem, load_sem, pair_send, pair_recv, out_send, out_recv, back_send, back_recv,
 ):
     core = lax.axis_index("dp")
     me = lax.axis_index("expert")
@@ -35,26 +36,38 @@
     def at(expert):
         return {"dp": core, "expert": expert}
 
-    def away(dz, j, sign):
-        dx, dy = j // YS, lax.rem(j, YS)
-        return (
-            lax.rem(z + sign * dz + ZS, ZS) * PLANE
-            + lax.rem(x + sign * dx + XS, XS) * YS
-            + lax.rem(y + sign * dy + YS, YS)
-        )
-
-    def blocks(chunk, act):
+    def blocks(chunk, sign, act):
         for i, dz in enumerate(CHUNKS[chunk]):
+            plane = lax.rem(z + sign * dz + ZS, ZS) * PLANE
             base = (2 * chunk + i) * PLANE
-
-            def step(j, carry):
-                act(base + j, dz, j)
+            if dz == 0:
+                for dy in range(1, YS):
+                    act(base + dy, plane + x * YS + ys[sign][dy])
+
+            def step(dx, carry):
+                line = plane + lax.rem(x + sign * dx + XS, XS) * YS
+                for dy in range(YS):
+                    act(base + dx * YS + dy, line + ys[sign][dy])
                 return carry
 
-            lax.fori_loop(1 if dz == 0 else 0, PLANE, step, 0)
-
-    def greet(k, dz, j):
-        pl.semaphore_signal(barrier, inc=1, device_id=at(away(dz, j, 1)), device_id_type=MESH)
+            lax.fori_loop(1 if dz == 0 else 0, XS, step, 0)
+
+    ys = {sign: [lax.rem(y + sign * dy + YS, YS) for dy in range(YS)] for sign in (1, -1)}
+
+    def greet(k, expert):
+        pl.semaphore_signal(barrier, inc=1, device_id=at(expert), device_id_type=MESH)
+
+    small = []
+    pieces = ((tokens_in, tokens), (gain_in, gain), (experts_in, experts), (slots_in, slots), (router_in, router))
+    for i, (source, target) in enumerate(pieces):
+        small.append(pltpu.make_async_copy(source, target, small_sem.at[i]))
+        small[-1].start()
+
+    barrier = pltpu.get_barrier_semaphore()
+    partner = {"dp": 1 - core, "expert": me}
+    pl.semaphore_signal(barrier, inc=1, device_id=partner, device_id_type=MESH)
+    for chunk in range(len(CHUNKS)):
+        blocks(chunk, 1, greet)
 
     loads = []
     for t in range(half):
@@ -64,12 +77,8 @@
     for copy in loads:
         copy.start()
 
-    barrier = pltpu.get_barrier_semaphore()
-    partner = {"dp": 1 - core, "expert": me}
-    pl.semaphore_signal(barrier, inc=1, device_id=partner, device_id_type=MESH)
-    for chunk in range(len(CHUNKS)):
-        blocks(chunk, greet)
-
+    for copy in small:
+        copy.wait()
     values = tokens[...].astype(jnp.float32)
     mean = jnp.mean(values, axis=1, keepdims=True)
     centred = values - mean
@@ -105,13 +114,13 @@
         )
 
     def dispatch(chunk):
-        def act(k, dz, j):
+        def act(k, expert):
             pltpu.make_async_remote_copy(
                 src_ref=send.at[k], dst_ref=recv.at[k], send_sem=out_send, recv_sem=out_recv.at[chunk],
-                device_id=at(away(dz, j, 1)), device_id_type=MESH,
+                device_id=at(expert), device_id_type=MESH,
             ).start()
 
-        blocks(chunk, act)
+        blocks(chunk, 1, act)
 
     pairs = []
     for chunk in range(len(CHUNKS)):
@@ -167,13 +176,13 @@
         lax.fori_loop(0, 2 * half, tile, 0)
         resp[first : first + CHUNK_BLOCKS] = acc[...].reshape(CHUNK_BLOCKS, CAP, -1).astype(jnp.bfloat16)
 
-        def answer(k, dz, j):
+        def answer(k, expert):
             pltpu.make_async_remote_copy(
                 src_ref=resp.at[k], dst_ref=back.at[k], send_sem=back_send, recv_sem=back_recv.at[chunk],
-                device_id=at(away(dz, j, -1)), device_id_type=MESH,
+                device_id=at(expert), device_id_type=MESH,
             ).start()
 
-        blocks(chunk, answer)
+        blocks(chunk, -1, answer)
     back[SELF] = resp[SELF]
 
     total = jnp.zeros(values.shape, jnp.float32)
@@ -183,28 +192,39 @@
         rows = back[first : first + CHUNK_BLOCKS].reshape(CHUNK_ROWS, -1)
         total = total + jnp.dot(onehot[chunk], rows, preferred_element_type=jnp.float32)
     update[...] = total.astype(jnp.bfloat16)
-    mixed[...] = (tokens[...].astype(jnp.float32) + gate[:, :1] * total).astype(jnp.bfloat16)
 
     for copy in pairs:
         copy.wait_send()
     for chunk in range(len(CHUNKS)):
         whole(send, recv, chunk, out_send, out_recv.at[chunk]).wait_send()
         whole(resp, back, chunk, back_send, back_recv.at[chunk]).wait_send()
+
+
+def finish(tokens, gate, total, mixed, update):
+    update[...] = total[...]
+    values = tokens[...].astype(jnp.float32)
+    mixed[...] = (values + gate[:, :1] * total[...].astype(jnp.float32)).astype(jnp.bfloat16)
 
 
 def per_device(tokens, ln_gain, router_weight, routes_expert, route_slot, w_in, w_out):
     count, width = tokens.shape
     half = w_in.shape[2] // TILE
     vmem = pl.BlockSpec(memory_space=pltpu.VMEM)
-    hbm = pl.BlockSpec(memory_space=pl.ANY)
+    hbm = pl.BlockSpec(memory_space=pltpu.MemorySpace.HBM)
     blocks = (EXPERTS, CAP, width)
     dma = pltpu.SemaphoreType.DMA
-    return pl.pallas_call(
+    shape = jax.ShapeDtypeStruct(tokens.shape, jnp.bfloat16)
+    total, gate = pl.pallas_call(
         kernel,
-        out_shape=(jax.ShapeDtypeStruct(tokens.shape, jnp.bfloat16),) * 2,
-        in_specs=[vmem] * 5 + [hbm] * 2,
+        out_shape=(pltpu.VMEM(tokens.shape, jnp.bfloat16), pltpu.VMEM((count, 128), jnp.float32)),
+        in_specs=[hbm] * 7,
         out_specs=(vmem, vmem),
         scratch_shapes=[
+            pltpu.VMEM(tokens.shape, jnp.bfloat16),
+            pltpu.VMEM((1, width), jnp.float32),
+            pltpu.VMEM(router_weight.shape, jnp.bfloat16),
+            pltpu.VMEM((1, count), jnp.int32),
+            pltpu.VMEM((1, count), jnp.int32),
             pltpu.VMEM(blocks, jnp.bfloat16),
             pltpu.VMEM(blocks, jnp.bfloat16),
             pltpu.VMEM(blocks, jnp.bfloat16),
@@ -213,18 +233,29 @@
             pltpu.VMEM((2 * half, TILE, width), jnp.bfloat16),
             pltpu.VMEM((count, width), jnp.bfloat16),
             pltpu.VMEM((CHUNK_ROWS, width), jnp.float32),
-            pltpu.VMEM((count, 128), jnp.float32),
             pltpu.VMEM((len(CHUNKS), count, CHUNK_ROWS), jnp.bfloat16),
-            dma((2, half)), dma((2, half)), dma((2, half)),
+            dma((5,)), dma((2, half)), dma((2, half)), dma((2, half)),
             dma, dma((len(CHUNKS),)), dma, dma((len(CHUNKS),)),
         ],
         compiler_params=pltpu.CompilerParams(
-            collective_id=0, has_side_effects=True, vmem_limit_bytes=56 * 1024 * 1024
+            collective_id=0, has_side_effects=True, vmem_limit_bytes=32 * 1024 * 1024
         ),
     )(
-        tokens, ln_gain.reshape(1, -1), router_weight,
-        routes_expert.reshape(1, -1), route_slot.reshape(1, -1), w_in, w_out,
+        *(
+            pltpu.with_memory_space_constraint(value, pltpu.MemorySpace.HBM)
+            for value in (
+                tokens, ln_gain.reshape(1, -1), router_weight,
+                routes_expert.reshape(1, -1), route_slot.reshape(1, -1), w_in, w_out,
+            )
+        )
     )
+    return pl.pallas_call(
+        finish,
+        out_shape=(shape, shape),
+        in_specs=[vmem] * 3,
+        out_specs=(vmem, vmem),
+        compiler_params=pltpu.CompilerParams(vmem_limit_bytes=8 * 1024 * 1024),
+    )(tokens, gate, total)
 
 
 def solution(mesh):

time: 69.7 us -> 63.7 us (0.914)
  local copies, waits for them, and re-layouts: 3.74 us -> 0.01 us
  Pallas kernels: 65.1 us -> 63 us
    unnamed x2, local copies, waits for them, and re-layouts: 3.74 us -> 0.01 us
    pallas_call x1 -> x2, Pallas kernels: 65.1 us -> 63 us  [the longest x1 61.9 us: per_device(): pl.pallas_call(kernel, out_shape=(pltpu.VMEM(tokens.shape, jnp.bfloat16),...]
where the time goes in v2:
time: 63.7 us
  Pallas kernels  63 us (99%)
  between operations  0.66 us (1%)
    pallas_call x1, Pallas kernels, per_device(): pl.pallas_call(kernel, out_shape=(pltpu.VMEM(tokens.shape, jnp.bfloat16),...  61.9 us

profile of v2, /device:TPU:1, one launch (start us, length us, event | category | flops | bytes accessed | tf_op | source)
XLA Modules:
  0.0 63.7 jit_solution(16083142726229230812)
XLA Ops:
  0.6 0.0 copy-start
  0.6 61.9 %shard_map.86 = (bf16[256,1024]{1,0:T(8,128)(2,1)S(1)}, f32[256,128]{1,0:T(8,128)S(1)}) custom-call(bf16[256,1024]{1,0:T(8,128)(2,1)} %tokens.1, f32[1,1024]{1,0:T(1,128)} %bitcast.3, bf16[1024,128]{1,0:T(8,128)(2,1)} %router_in.1, s32[1,256]{1,0:T(1,128)} %bitcast.4, s32[1,256]{1,0:T(1,128)} %bitcast.5, bf16[1,1024,2048]{2,1,0:T(8,128)(2,1)} %w_in.1, ...), custom_call_target="tpu_custom_call" | custom-call | tf_op jit(solution)/shard_map/pallas_call | solution.py:217
  62.5 0.0 copy-done
  62.5 1.1 %shard_map.87 = (bf16[256,1024]{1,0:T(8,128)(2,1)}, bf16[256,1024]{1,0:T(8,128)(2,1)}) custom-call(bf16[256,1024]{1,0:T(8,128)(2,1)S(1)} %copy-done, f32[256,128]{1,0:T(8,128)S(1)} %get-tuple-element.4.gate, bf16[256,1024]{1,0:T(8,128)(2,1)S(1)} %get-tuple-element.5.total), custom_call_target="tpu_custom_call" | custom-call | tf_op jit(solution)/shard_map/pallas_call | solution.py:252
Async XLA Ops:
  0.6 61.9 %copy-start = (bf16[256,1024]{1,0:T(8,128)(2,1)S(1)}, bf16[256,1024]{1,0:T(8,128)(2,1)}, u32[]{:S(2)}) copy-start(bf16[256,1024]{1,0:T(8,128)(2,1)} %tokens.1) | copy-start | bytes 1572868

commit v3 on v2

--- a/solution.py
+++ b/solution.py
@@ -12,7 +12,7 @@
 PLANE = XS * YS
 EXPERTS = ZS * PLANE
 SLOTS = EXPERTS * CAP
-CHUNKS = ((3, 5), (2, 6), (4, 0), (1, 7))
+CHUNKS = ((2, 6), (4, 0), (3, 5), (1, 7))
 ORDER = tuple(dz for pair in CHUNKS for dz in pair)
 SELF = ORDER.index(0) * PLANE
 CHUNK_BLOCKS = 2 * PLANE
@@ -36,7 +36,7 @@
     def at(expert):
         return {"dp": core, "expert": expert}
 
-    def blocks(chunk, sign, act):
+    def blocks(chunk, sign, act, far_first=False):
         for i, dz in enumerate(CHUNKS[chunk]):
             plane = lax.rem(z + sign * dz + ZS, ZS) * PLANE
             base = (2 * chunk + i) * PLANE
@@ -44,13 +44,16 @@
                 for dy in range(1, YS):
                     act(base + dy, plane + x * YS + ys[sign][dy])
 
-            def step(dx, carry):
+            def step(s, carry):
+                t = XS - 1 - s
+                dx = t + t // 2 - 2 * (t // 3) if far_first else s
                 line = plane + lax.rem(x + sign * dx + XS, XS) * YS
-                for dy in range(YS):
+                for dy in (2, 1, 3, 0) if far_first else range(YS):
                     act(base + dx * YS + dy, line + ys[sign][dy])
                 return carry
 
-            lax.fori_loop(1 if dz == 0 else 0, XS, step, 0)
+            first = 1 if dz == 0 else 0
+            lax.fori_loop(0 if far_first else first, XS - first if far_first else XS, step, 0)
 
     ys = {sign: [lax.rem(y + sign * dy + YS, YS) for dy in range(YS)] for sign in (1, -1)}
 
@@ -67,7 +70,7 @@
     partner = {"dp": 1 - core, "expert": me}
     pl.semaphore_signal(barrier, inc=1, device_id=partner, device_id_type=MESH)
     for chunk in range(len(CHUNKS)):
-        blocks(chunk, 1, greet)
+        blocks((1, 2, 0, 3)[chunk], 1, greet, True)
 
     loads = []
     for t in range(half):
@@ -182,7 +185,7 @@
                 device_id=at(expert), device_id_type=MESH,
             ).start()
 
-        blocks(chunk, -1, answer)
+        blocks(chunk, -1, answer, True)
     back[SELF] = resp[SELF]
 
     total = jnp.zeros(values.shape, jnp.float32)
@@ -252,8 +255,9 @@
     return pl.pallas_call(
         finish,
         out_shape=(shape, shape),
-        in_specs=[vmem] * 3,
-        out_specs=(vmem, vmem),
+        grid=(2,),
+        in_specs=[pl.BlockSpec((count // 2, n), lambda i: (i, 0)) for n in (width, 128, width)],
+        out_specs=(pl.BlockSpec((count // 2, width), lambda i: (i, 0)),) * 2,
         compiler_params=pltpu.CompilerParams(vmem_limit_bytes=8 * 1024 * 1024),
     )(tokens, gate, total)
 

time: 63.7 us -> 62.3 us (0.978)
  Pallas kernels: 63 us -> 61.5 us
    pallas_call x1, Pallas kernels: 61.9 us -> 60.5 us  [per_device(): pl.pallas_call(kernel, out_shape=(pltpu.VMEM(tokens.shape, jnp.bfloat16),...]
where the time goes in v3:
time: 62.3 us; the launch traced here: 62.2 us
  Pallas kernels  61.5 us (99%)
  between operations  0.66 us (1%)
    pallas_call x1, Pallas kernels, per_device(): pl.pallas_call(kernel, out_shape=(pltpu.VMEM(tokens.shape, jnp.bfloat16),...  60.5 us

profile of v3, /device:TPU:1, one launch (start us, length us, event | category | flops | bytes accessed | tf_op | source)
XLA Modules:
  0.0 62.2 jit_solution(10292955500646406186)
XLA Ops:
  0.6 0.0 copy-start
  0.6 60.5 %shard_map.86 = (bf16[256,1024]{1,0:T(8,128)(2,1)S(1)}, f32[256,128]{1,0:T(8,128)S(1)}) custom-call(bf16[256,1024]{1,0:T(8,128)(2,1)} %tokens.1, f32[1,1024]{1,0:T(1,128)} %bitcast.3, bf16[1024,128]{1,0:T(8,128)(2,1)} %router_in.1, s32[1,256]{1,0:T(1,128)} %bitcast.4, s32[1,256]{1,0:T(1,128)} %bitcast.5, bf16[1,1024,2048]{2,1,0:T(8,128)(2,1)} %w_in.1, ...), custom_call_target="tpu_custom_call" | custom-call | tf_op jit(solution)/shard_map/pallas_call | solution.py:220
  61.1 0.0 copy-done
  61.2 1.1 %shard_map.87 = (bf16[256,1024]{1,0:T(8,128)(2,1)}, bf16[256,1024]{1,0:T(8,128)(2,1)}) custom-call(bf16[256,1024]{1,0:T(8,128)(2,1)S(1)} %copy-done, f32[256,128]{1,0:T(8,128)S(1)} %get-tuple-element.4.gate, bf16[256,1024]{1,0:T(8,128)(2,1)S(1)} %get-tuple-element.5.total), custom_call_target="tpu_custom_call" | custom-call | tf_op jit(solution)/shard_map/pallas_call | solution.py:255
Async XLA Ops:
  0.6 60.5 %copy-start = (bf16[256,1024]{1,0:T(8,128)(2,1)S(1)}, bf16[256,1024]{1,0:T(8,128)(2,1)}, u32[]{:S(2)}) copy-start(bf16[256,1024]{1,0:T(8,128)(2,1)} %tokens.1) | copy-start | bytes 1572868

commit v4 on v3

--- a/solution.py
+++ b/solution.py
@@ -15,6 +15,7 @@
 CHUNKS = ((2, 6), (4, 0), (3, 5), (1, 7))
 ORDER = tuple(dz for pair in CHUNKS for dz in pair)
 SELF = ORDER.index(0) * PLANE
+SELF_CHUNK = ORDER.index(0) // 2
 CHUNK_BLOCKS = 2 * PLANE
 CHUNK_ROWS = CHUNK_BLOCKS * CAP
 TILE = 512
@@ -26,7 +27,7 @@
     update, gate,
     tokens, gain, router, experts, slots,
     send, recv, resp, back, win, wout, normed, acc, onehot,
-    small_sem, load_sem, pair_send, pair_recv, out_send, out_recv, back_send, back_recv,
+    ready, small_sem, load_sem, pair_send, pair_recv, out_send, out_recv, back_send, back_recv,
 ):
     core = lax.axis_index("dp")
     me = lax.axis_index("expert")
@@ -36,11 +37,16 @@
     def at(expert):
         return {"dp": core, "expert": expert}
 
-    def blocks(chunk, sign, act, far_first=False):
+    def blocks(chunk, sign, act, far_first=False, column=True, only=tuple(range(ZS))):
         for i, dz in enumerate(CHUNKS[chunk]):
+            if dz not in only:
+                continue
             plane = lax.rem(z + sign * dz + ZS, ZS) * PLANE
             base = (2 * chunk + i) * PLANE
-            if dz == 0:
+            whole_column = column and dz != 0
+            if not column and dz != 0:
+                pl.semaphore_wait(ready.at[dz], 1)
+            if not whole_column:
                 for dy in range(1, YS):
                     act(base + dy, plane + x * YS + ys[sign][dy])
 
@@ -52,9 +58,10 @@
                     act(base + dx * YS + dy, line + ys[sign][dy])
                 return carry
 
-            first = 1 if dz == 0 else 0
+            first = 0 if whole_column else 1
             lax.fori_loop(0 if far_first else first, XS - first if far_first else XS, step, 0)
 
+    columns = tuple((ORDER.index(dz) * PLANE, dz, lax.rem(z + dz, ZS) * PLANE + x * YS + y) for dz in ORDER if dz)
     ys = {sign: [lax.rem(y + sign * dy + YS, YS) for dy in range(YS)] for sign in (1, -1)}
 
     def greet(k, expert):
@@ -69,8 +76,9 @@
     barrier = pltpu.get_barrier_semaphore()
     partner = {"dp": 1 - core, "expert": me}
     pl.semaphore_signal(barrier, inc=1, device_id=partner, device_id_type=MESH)
-    for chunk in range(len(CHUNKS)):
-        blocks((1, 2, 0, 3)[chunk], 1, greet, True)
+    for k, dz, peer in columns:
+        greet(k, peer)
+    blocks(SELF_CHUNK, 1, greet, True, False, (0,))
 
     loads = []
     for t in range(half):
@@ -106,7 +114,9 @@
         first = chunk * CHUNK_BLOCKS
         send[first : first + CHUNK_BLOCKS] = picked.reshape(CHUNK_BLOCKS, CAP, -1).astype(jnp.bfloat16)
 
-    pl.semaphore_wait(barrier, EXPERTS)
+    pl.semaphore_wait(barrier, len(columns) + PLANE)
+    for k, dz, peer in columns:
+        pl.semaphore_signal(ready.at[ZS - dz], inc=1, device_id=at(peer), device_id_type=MESH)
 
     def pair_copy(w, t, which):
         dst = (win, wout)[which].at[half + t]
@@ -123,11 +133,13 @@
                 device_id=at(expert), device_id_type=MESH,
             ).start()
 
-        blocks(chunk, 1, act)
-
+        return act
+
+    for k, dz, peer in columns:
+        dispatch(ORDER.index(dz) // 2)(k, peer)
     pairs = []
     for chunk in range(len(CHUNKS)):
-        dispatch(chunk)
+        blocks(chunk, 1, dispatch(chunk), column=False)
         if chunk == 0:
             pairs = [pair_copy((w_in, w_out)[s], t, s) for t in range(half) for s in (0, 1)]
             for copy in pairs:
@@ -162,9 +174,6 @@
 
     for chunk in range(len(CHUNKS)):
         whole(send, recv, chunk, out_send, out_recv.at[chunk]).wait_recv()
-        if chunk == 0:
-            for copy in pairs:
-                copy.wait_recv()
         first = chunk * CHUNK_BLOCKS
         here = recv[first : first + CHUNK_BLOCKS].reshape(CHUNK_ROWS, -1)
         acc[...] = jnp.zeros_like(acc)
@@ -176,7 +185,14 @@
             acc[...] += jnp.dot(hidden, wout[t], preferred_element_type=jnp.float32)
             return carry
 
-        lax.fori_loop(0, 2 * half, tile, 0)
+        if chunk == 0:
+            lax.fori_loop(0, half, tile, 0)
+            for t in range(half):
+                for copy in pairs[2 * t : 2 * t + 2]:
+                    copy.wait_recv()
+                tile(half + t, 0)
+        else:
+            lax.fori_loop(0, 2 * half, tile, 0)
         resp[first : first + CHUNK_BLOCKS] = acc[...].reshape(CHUNK_BLOCKS, CAP, -1).astype(jnp.bfloat16)
 
         def answer(k, expert):
@@ -237,7 +253,7 @@
             pltpu.VMEM((count, width), jnp.bfloat16),
             pltpu.VMEM((CHUNK_ROWS, width), jnp.float32),
             pltpu.VMEM((len(CHUNKS), count, CHUNK_ROWS), jnp.bfloat16),
-            dma((5,)), dma((2, half)), dma((2, half)), dma((2, half)),
+            pltpu.SemaphoreType.REGULAR((ZS,)), dma((5,)), dma((2, half)), dma((2, half)), dma((2, half)),
             dma, dma((len(CHUNKS),)), dma, dma((len(CHUNKS),)),
         ],
         compiler_params=pltpu.CompilerParams(

time: 62.3 us -> 61.2 us (0.982)
  Pallas kernels: 61.5 us -> 60.5 us
    pallas_call x1, Pallas kernels: 60.5 us -> 59.4 us  [per_device(): pl.pallas_call(kernel, out_shape=(pltpu.VMEM(tokens.shape, jnp.bfloat16),...]
where the time goes in v4:
time: 61.2 us; the launch traced here: 61.1 us
  Pallas kernels  60.5 us (99%)
  between operations  0.66 us (1%)
    pallas_call x1, Pallas kernels, per_device(): pl.pallas_call(kernel, out_shape=(pltpu.VMEM(tokens.shape, jnp.bfloat16),...  59.4 us

profile of v4, /device:TPU:1, one launch (start us, length us, event | category | flops | bytes accessed | tf_op | source)
XLA Modules:
  0.0 61.1 jit_solution(11668471684365458740)
XLA Ops:
  0.6 0.0 copy-start
  0.6 59.4 %shard_map.86 = (bf16[256,1024]{1,0:T(8,128)(2,1)S(1)}, f32[256,128]{1,0:T(8,128)S(1)}) custom-call(bf16[256,1024]{1,0:T(8,128)(2,1)} %tokens.1, f32[1,1024]{1,0:T(1,128)} %bitcast.3, bf16[1024,128]{1,0:T(8,128)(2,1)} %router_in.1, s32[1,256]{1,0:T(1,128)} %bitcast.4, s32[1,256]{1,0:T(1,128)} %bitcast.5, bf16[1,1024,2048]{2,1,0:T(8,128)(2,1)} %w_in.1, ...), custom_call_target="tpu_custom_call" | custom-call | tf_op jit(solution)/shard_map/pallas_call | solution.py:236
  60.1 0.0 copy-done
  60.1 1.1 %shard_map.87 = (bf16[256,1024]{1,0:T(8,128)(2,1)}, bf16[256,1024]{1,0:T(8,128)(2,1)}) custom-call(bf16[256,1024]{1,0:T(8,128)(2,1)S(1)} %copy-done, f32[256,128]{1,0:T(8,128)S(1)} %get-tuple-element.4.gate, bf16[256,1024]{1,0:T(8,128)(2,1)S(1)} %get-tuple-element.5.total), custom_call_target="tpu_custom_call" | custom-call | tf_op jit(solution)/shard_map/pallas_call | solution.py:271
Async XLA Ops:
  0.6 59.4 %copy-start = (bf16[256,1024]{1,0:T(8,128)(2,1)S(1)}, bf16[256,1024]{1,0:T(8,128)(2,1)}, u32[]{:S(2)}) copy-start(bf16[256,1024]{1,0:T(8,128)(2,1)} %tokens.1) | copy-start | bytes 1572868

commit v5 on v4

--- a/solution.py
+++ b/solution.py
@@ -12,7 +12,7 @@
 PLANE = XS * YS
 EXPERTS = ZS * PLANE
 SLOTS = EXPERTS * CAP
-CHUNKS = ((2, 6), (4, 0), (3, 5), (1, 7))
+CHUNKS = ((2, 6), (3, 5), (0, 4), (1, 7))
 ORDER = tuple(dz for pair in CHUNKS for dz in pair)
 SELF = ORDER.index(0) * PLANE
 SELF_CHUNK = ORDER.index(0) // 2
@@ -186,13 +186,13 @@
             return carry
 
         if chunk == 0:
-            lax.fori_loop(0, half, tile, 0)
+            lax.fori_loop(0, half, tile, 0, unroll=2)
             for t in range(half):
                 for copy in pairs[2 * t : 2 * t + 2]:
                     copy.wait_recv()
                 tile(half + t, 0)
         else:
-            lax.fori_loop(0, 2 * half, tile, 0)
+            lax.fori_loop(0, 2 * half, tile, 0, unroll=2)
         resp[first : first + CHUNK_BLOCKS] = acc[...].reshape(CHUNK_BLOCKS, CAP, -1).astype(jnp.bfloat16)
 
         def answer(k, expert):

time: 61.2 us -> 61.1 us (level)
  no operation moved by 1% of the time
where the time goes in v5:
time: 61.1 us; the launch traced here: 61 us
  Pallas kernels  60.4 us (99%)
  between operations  0.66 us (1%)
    pallas_call x1, Pallas kernels, per_device(): pl.pallas_call(kernel, out_shape=(pltpu.VMEM(tokens.shape, jnp.bfloat16),...  59.3 us

profile of v5, /device:TPU:1, one launch (start us, length us, event | category | flops | bytes accessed | tf_op | source)
XLA Modules:
  0.0 61.0 jit_solution(7069293013989252751)
XLA Ops:
  0.6 0.0 copy-start
  0.6 59.3 %shard_map.86 = (bf16[256,1024]{1,0:T(8,128)(2,1)S(1)}, f32[256,128]{1,0:T(8,128)S(1)}) custom-call(bf16[256,1024]{1,0:T(8,128)(2,1)} %tokens.1, f32[1,1024]{1,0:T(1,128)} %bitcast.3, bf16[1024,128]{1,0:T(8,128)(2,1)} %router_in.1, s32[1,256]{1,0:T(1,128)} %bitcast.4, s32[1,256]{1,0:T(1,128)} %bitcast.5, bf16[1,1024,2048]{2,1,0:T(8,128)(2,1)} %w_in.1, ...), custom_call_target="tpu_custom_call" | custom-call | tf_op jit(solution)/shard_map/pallas_call | solution.py:236
  60.0 0.0 copy-done
  60.0 1.1 %shard_map.87 = (bf16[256,1024]{1,0:T(8,128)(2,1)}, bf16[256,1024]{1,0:T(8,128)(2,1)}) custom-call(bf16[256,1024]{1,0:T(8,128)(2,1)S(1)} %copy-done, f32[256,128]{1,0:T(8,128)S(1)} %get-tuple-element.4.gate, bf16[256,1024]{1,0:T(8,128)(2,1)S(1)} %get-tuple-element.5.total), custom_call_target="tpu_custom_call" | custom-call | tf_op jit(solution)/shard_map/pallas_call | solution.py:271
Async XLA Ops:
  0.6 59.3 %copy-start = (bf16[256,1024]{1,0:T(8,128)(2,1)S(1)}, bf16[256,1024]{1,0:T(8,128)(2,1)}, u32[]{:S(2)}) copy-start(bf16[256,1024]{1,0:T(8,128)(2,1)} %tokens.1) | copy-start | bytes 1572868

commit v6 on v5

--- a/solution.py
+++ b/solution.py
@@ -80,14 +80,6 @@
         greet(k, peer)
     blocks(SELF_CHUNK, 1, greet, True, False, (0,))
 
-    loads = []
-    for t in range(half):
-        cols = pl.ds(t * TILE, TILE)
-        loads.append(pltpu.make_async_copy(w_in.at[0, :, cols], win.at[t], load_sem.at[0, t]))
-        loads.append(pltpu.make_async_copy(w_out.at[0, cols, :], wout.at[t], load_sem.at[1, t]))
-    for copy in loads:
-        copy.start()
-
     for copy in small:
         copy.wait()
     values = tokens[...].astype(jnp.float32)
@@ -145,6 +137,14 @@
             for copy in pairs:
                 copy.start()
     recv[SELF] = send[SELF]
+
+    loads = []
+    for t in range(half):
+        cols = pl.ds(t * TILE, TILE)
+        loads.append(pltpu.make_async_copy(w_in.at[0, :, cols], win.at[t], load_sem.at[0, t]))
+        loads.append(pltpu.make_async_copy(w_out.at[0, cols, :], wout.at[t], load_sem.at[1, t]))
+    for copy in loads:
+        copy.start()
 
     eye = lax.broadcasted_iota(jnp.int32, (count, count), 0) == lax.broadcasted_iota(jnp.int32, (count, count), 1)
 

time: 61.1 us -> 61.1 us (level)
  no operation moved by 1% of the time
where the time goes in v6:
time: 61.1 us; the launch traced here: 61 us
  Pallas kernels  60.4 us (99%)
  between operations  0.66 us (1%)
    pallas_call x1, Pallas kernels, per_device(): pl.pallas_call(kernel, out_shape=(pltpu.VMEM(tokens.shape, jnp.bfloat16),...  59.3 us

profile of v6, /device:TPU:1, one launch (start us, length us, event | category | flops | bytes accessed | tf_op | source)
XLA Modules:
  0.0 61.0 jit_solution(9055100594666424410)
XLA Ops:
  0.6 0.0 copy-start
  0.6 59.3 %shard_map.86 = (bf16[256,1024]{1,0:T(8,128)(2,1)S(1)}, f32[256,128]{1,0:T(8,128)S(1)}) custom-call(bf16[256,1024]{1,0:T(8,128)(2,1)} %tokens.1, f32[1,1024]{1,0:T(1,128)} %bitcast.3, bf16[1024,128]{1,0:T(8,128)(2,1)} %router_in.1, s32[1,256]{1,0:T(1,128)} %bitcast.4, s32[1,256]{1,0:T(1,128)} %bitcast.5, bf16[1,1024,2048]{2,1,0:T(8,128)(2,1)} %w_in.1, ...), custom_call_target="tpu_custom_call" | custom-call | tf_op jit(solution)/shard_map/pallas_call | solution.py:236
  60.0 0.0 copy-done
  60.0 1.1 %shard_map.87 = (bf16[256,1024]{1,0:T(8,128)(2,1)}, bf16[256,1024]{1,0:T(8,128)(2,1)}) custom-call(bf16[256,1024]{1,0:T(8,128)(2,1)S(1)} %copy-done, f32[256,128]{1,0:T(8,128)S(1)} %get-tuple-element.4.gate, bf16[256,1024]{1,0:T(8,128)(2,1)S(1)} %get-tuple-element.5.total), custom_call_target="tpu_custom_call" | custom-call | tf_op jit(solution)/shard_map/pallas_call | solution.py:271
Async XLA Ops:
  0.6 59.3 %copy-start = (bf16[256,1024]{1,0:T(8,128)(2,1)S(1)}, bf16[256,1024]{1,0:T(8,128)(2,1)}, u32[]{:S(2)}) copy-start(bf16[256,1024]{1,0:T(8,128)(2,1)} %tokens.1) | copy-start | bytes 1572868
